TPU v7x, 32 devices: a whole 2x2x4 slice. The times are simulated.
32 devices in a mesh: walk: 8 (over z, x), chol: 4 (over y, core).
Axes of the slice: x: 2, y: 2, z: 4, core: 2. Of those that a mesh axis runs over, the one named last changes fastest.
Arguments:
- orbitals: bfloat16 [8, 400, 2048], P('walk', None, 'chol'), may hold values from -4 to 4
- intersection_inv: bfloat16 [8, 400, 400], P('walk'), may hold values from -0.18 to 0.18
- interp: bfloat16 [2048, 2048], P(None, 'chol'), may hold values from -0.079549513 to 0.079549513
- occ_interp: bfloat16 [400, 2048], P(None, 'chol'), may hold values from -0.18 to 0.18
- chol_factors: bfloat16 [2048, 2048], P('chol', 'walk'), may hold values from -2 to 2
- fields: float32 [8, 2048], P(None, 'walk'), may hold values from -4 to 4
Outputs:
- new_orbitals: bfloat16 [8, 400, 2048], P('walk', None, 'chol')
- force_bias: float32 [8, 2048], P(None, 'walk')
All inputs are finite; a program needn't handle non-finite values.
Results may differ from a plain program's by a relative error of at most 0.017.
Values may be sent and summed in bfloat16 or wider, within the bound.
A program may use at most 64 MiB of HBM per device.

v0:
```python
import jax
import jax.numpy as jnp
from jax import lax
from jax.sharding import PartitionSpec as P

TERMS = 4
time_root = 2.2


def on_device(orbitals, intersection_inv, interp, occ_interp, chol_factors, fields):
    walkers_here, electrons, basis_here = orbitals.shape
    piece = lax.all_gather(orbitals, "chol", axis=2, tiled=True)
    green = jnp.einsum(
        "wij,wjm->wim", intersection_inv, piece, preferred_element_type=jnp.float32
    ).astype(jnp.bfloat16)
    projected = jnp.einsum("wim,mp->wip", green, interp, preferred_element_type=jnp.float32)
    applied = jnp.einsum("wim,mp->wip", piece, interp, preferred_element_type=jnp.float32)
    projected, current = (projected, applied)
    weights = jnp.sum(occ_interp.astype(jnp.float32)[None] * projected, axis=1)
    factors = chol_factors.astype(jnp.float32)
    all_weights = lax.all_gather(weights, "walk", axis=0, tiled=True)
    partial_bias = jnp.dot(all_weights, factors, precision=lax.Precision.HIGHEST)
    force_bias = lax.psum(partial_bias, "chol")
    coeff = time_root * (fields - force_bias)
    field_part = jnp.dot(coeff, factors.T, precision=lax.Precision.HIGHEST)
    scales = lax.psum_scatter(field_part, "walk", scatter_dimension=0, tiled=True)
    total = orbitals.astype(jnp.float32)
    for order in range(1, TERMS + 1):
        mixed = (current * scales[:, None, :] / order).astype(jnp.bfloat16)
        partial_value = jnp.einsum("wnp,mp->wnm", mixed, interp, preferred_element_type=jnp.float32)
        term_whole = lax.psum(partial_value.astype(jnp.bfloat16), "chol")
        offset = lax.axis_index("chol") * basis_here
        term_local = lax.dynamic_slice_in_dim(term_whole, offset, basis_here, 2)
        total = total + term_local.astype(jnp.float32)
        if order < TERMS:
            current = jnp.einsum(
                "wnm,mp->wnp", term_whole, interp, preferred_element_type=jnp.float32
            )
    return (total.astype(jnp.bfloat16), force_bias)


def solution(mesh):
    placed = (
        P("walk", None, "chol"),
        P("walk", None, None),
        P(None, "chol"),
        P(None, "chol"),
        P("chol", "walk"),
        P(None, "walk"),
    )
    return jax.shard_map(
        on_device,
        mesh=mesh,
        in_specs=placed,
        out_specs=(P("walk", None, "chol"), P(None, "walk")),
        check_vma=False,
    )
```

profile of v0, /device:TPU:0, one launch (start us, length us, event | category | flops | bytes accessed | tf_op | source)
XLA Modules:
  0.0 304.3 jit_solution(10062563972776809825)
XLA Ops:
  7.2 0.0 copy-start
  7.2 0.0 all-gather.4.cloned.1.call-start
  7.2 0.7 all-gather.4.cloned.1.call-update
  7.9 0.0 all-reduce.6.cloned.1.call-start
  8.0 1.2 dynamic-slice
  9.2 0.0 copy-start.2
  9.2 0.0 copy-start.4
  9.2 23.1 %all-gather.4.cloned.1.call-done = bf16[1,400,2048]{2,1,0:T(8,128)(2,1)} async-done(((bf16[1,400,512]{2,1,0:T(8,128)(2,1)}), bf16[1,400,2048]{2,1,0:T(8,128)(2,1)}) %all-gather.4.cloned.1.call-update) | async-done | bytes 1638416 | tf_op jit(solution)/shard_map/all_gather | solution.py:12
  32.3 0.0 copy-done
  32.3 3.5 %fusion.46 = f32[512]{0:T(512)S(1)} fusion(bf16[2048,512]{1,0:T(8,128)(2,1)S(1)} %copy-done, bf16[1,400,2048]{2,1,0:T(8,128)(2,1)} %all-gather.4.cloned.1.call-done, bf16[400,512]{1,0:T(8,128)(2,1)} %param.9, bf16[1,400,400]{2,1,0:T(8,128)(2,1)} %param.7), kind=kOutput, calls=%fused_computation.30 | convolution fusion | flops 1495653888 | bytes 4467200 | tf_op jit(solution)/shard_map/wim,mp->wip/dot_general | solution.py:16
  35.8 26.2 %all-gather.1 = f32[8,1,512]{2,1,0:T(1,128)S(1)} all-gather(f32[1,1,512]{2,1,0:T(1,128)S(1)} %bitcast.75), channel_id=2, replica_groups=mesh['walk'=8,'chol'=4] {'walk'}, dimensions={0}, use_global_device_ids=true | all-gather | bytes 18432 | tf_op jit(solution)/shard_map/all_gather | solution.py:21
  62.0 0.0 copy-done.2
  62.0 0.2 fusion.66
  62.2 6.1 %psum.35 = f32[8,256]{1,0:T(8,128)S(1)} all-reduce(f32[8,256]{1,0:T(8,128)S(1)} %fusion.66), channel_id=1, replica_groups=mesh['walk'=8,'chol'=4] {'chol'}, use_global_device_ids=true, to_apply=%region_1.0 | all-reduce | flops 2048 | bytes 16384 | tf_op jit(solution)/shard_map/psum | solution.py:23
  68.3 0.0 copy-done.4
  68.3 0.0 copy-start.3
  68.3 0.3 fusion.69
  68.6 35.5 %all-reduce = f32[8,512]{1,0:T(8,128)S(1)} all-reduce(f32[8,512]{1,0:T(8,128)S(1)} %fusion.69), channel_id=3, replica_groups=mesh['walk'=8,'chol'=4] {'walk'}, use_global_device_ids=true, to_apply=%region_2.0.clone | all-reduce | flops 4096 | bytes 32768
  104.1 0.6 constant_dynamic-slice_fusion
  104.8 4.5 %fusion = bf16[1,400,2048]{2,1,0:T(8,128)(2,1)} fusion(bf16[2048,512]{1,0:T(8,128)(2,1)S(1)} %copy-done, bf16[1,400,2048]{2,1,0:T(8,128)(2,1)} %all-gather.4.cloned.1.call-done, f32[512]{0:T(512)S(1)} %bitcast.76), kind=kOutput, calls=%fused_computation.5 | convolution fusion | flops 1678950400 | bytes 5376000 | tf_op jit(solution)/shard_map/wnp,mp->wnm/dot_general | solution.py:30
  109.3 0.0 copy-done.3
  109.3 0.0 all-reduce.6.cloned.1.call-update
  109.3 0.0 all-reduce.8.cloned.1.call-start
  109.4 40.0 %all-reduce.6.cloned.1.call-done = bf16[1,400,2048]{2,1,0:T(8,128)(2,1)} async-done(((bf16[1,400,2048]{2,1,0:T(8,128)(2,1)}), bf16[1,400,2048]{2,1,0:T(8,128)(2,1)}) %all-reduce.6.cloned.1.call-update) | async-done | bytes 1638416 | tf_op jit(solution)/shard_map/psum | solution.py:31
  149.4 4.5 %fusion.1 = bf16[1,400,2048]{2,1,0:T(8,128)(2,1)} fusion(bf16[2048,512]{1,0:T(8,128)(2,1)S(1)} %copy-done, bf16[1,400,2048]{2,1,0:T(8,128)(2,1)} %all-reduce.6.cloned.1.call-done, f32[512]{0:T(512)S(1)} %bitcast.77), kind=kOutput, calls=%fused_computation.6 | convolution fusion | flops 1679155200 | bytes 5376000 | tf_op jit(solution)/shard_map/wnp,mp->wnm/dot_general | solution.py:30
  153.9 0.0 all-reduce.8.cloned.1.call-update
  153.9 0.0 all-reduce.10.cloned.1.call-start
  154.0 44.1 %all-reduce.8.cloned.1.call-done = bf16[1,400,2048]{2,1,0:T(8,128)(2,1)} async-done(((bf16[1,400,2048]{2,1,0:T(8,128)(2,1)}), bf16[1,400,2048]{2,1,0:T(8,128)(2,1)}) %all-reduce.8.cloned.1.call-update) | async-done | bytes 1638416 | tf_op jit(solution)/shard_map/psum | solution.py:31
  198.0 4.5 %fusion.2 = bf16[1,400,2048]{2,1,0:T(8,128)(2,1)} fusion(bf16[2048,512]{1,0:T(8,128)(2,1)S(1)} %copy-done, bf16[1,400,2048]{2,1,0:T(8,128)(2,1)} %all-reduce.8.cloned.1.call-done, f32[512]{0:T(512)S(1)} %bitcast.78), kind=kOutput, calls=%fused_computation.7 | convolution fusion | flops 1679155200 | bytes 5376000 | tf_op jit(solution)/shard_map/wnp,mp->wnm/dot_general | solution.py:30
  202.6 0.0 all-reduce.10.cloned.1.call-update
  202.6 0.0 all-reduce.12.cloned.1.call-start
  202.6 44.1 %all-reduce.10.cloned.1.call-done = bf16[1,400,2048]{2,1,0:T(8,128)(2,1)} async-done(((bf16[1,400,2048]{2,1,0:T(8,128)(2,1)}), bf16[1,400,2048]{2,1,0:T(8,128)(2,1)}) %all-reduce.10.cloned.1.call-update) | async-done | bytes 1638416 | tf_op jit(solution)/shard_map/psum | solution.py:31
  246.7 4.5 %fusion.3 = bf16[1,400,2048]{2,1,0:T(8,128)(2,1)} fusion(bf16[2048,512]{1,0:T(8,128)(2,1)S(1)} %copy-done, bf16[1,400,2048]{2,1,0:T(8,128)(2,1)} %all-reduce.10.cloned.1.call-done, f32[512]{0:T(512)S(1)} %bitcast.79), kind=kOutput, calls=%fused_computation.8 | convolution fusion | flops 1679155200 | bytes 5376000 | tf_op jit(solution)/shard_map/wnp,mp->wnm/dot_general | solution.py:30
  251.2 0.0 copy-start.1
  251.2 0.0 all-reduce.12.cloned.1.call-update
  251.3 44.1 %all-reduce.12.cloned.1.call-done = bf16[1,400,2048]{2,1,0:T(8,128)(2,1)} async-done(((bf16[1,400,2048]{2,1,0:T(8,128)(2,1)}), bf16[1,400,2048]{2,1,0:T(8,128)(2,1)}) %all-reduce.12.cloned.1.call-update) | async-done | bytes 1638416 | tf_op jit(solution)/shard_map/psum | solution.py:31
  295.4 0.0 copy-done.1
  295.4 2.4 add_convert_fusion
Async XLA Ops:
  7.2 25.1 %copy-start = (bf16[2048,512]{1,0:T(8,128)(2,1)S(1)}, bf16[2048,512]{1,0:T(8,128)(2,1)}, u32[]{:S(2)}) copy-start(bf16[2048,512]{1,0:T(8,128)(2,1)} %param.8) | copy-start | bytes 6291460
  7.2 25.1 %all-gather.4.cloned.1.call-start = ((), (), s32[]{:S(2)}) async-start(), calls=%async_computation | async-start | bytes 2048000 | tf_op jit(solution)/shard_map/all_gather | solution.py:12
  7.9 141.5 %all-reduce.6.cloned.1.call-start = ((), (), s32[]{:S(2)}) async-start(), calls=%async_computation.1 | async-start | bytes 3276800 | tf_op jit(solution)/shard_map/psum | solution.py:31
  9.2 52.8 %copy-start.2 = (bf16[512,256]{1,0:T(8,128)(2,1)S(1)}, bf16[512,256]{1,0:T(8,128)(2,1)}, u32[]{:S(2)}) copy-start(bf16[512,256]{1,0:T(8,128)(2,1)} %param.10) | copy-start | bytes 786436
  9.2 59.1 %copy-start.4 = (f32[8,256]{1,0:T(8,128)S(1)}, f32[8,256]{1,0:T(8,128)}, u32[]{:S(2)}) copy-start(f32[8,256]{1,0:T(8,128)} %param.11) | copy-start | bytes 24580
  68.3 41.0 %copy-start.3 = (f32[8,256]{1,0:T(8,128)}, f32[8,256]{1,0:T(8,128)S(1)}, u32[]{:S(2)}) copy-start(f32[8,256]{1,0:T(8,128)S(1)} %psum.35) | copy-start | bytes 24580
  109.3 88.7 %all-reduce.8.cloned.1.call-start = ((), (), s32[]{:S(2)}) async-start(), calls=%async_computation.2 | async-start | bytes 3276800 | tf_op jit(solution)/shard_map/psum | solution.py:31
  153.9 92.8 %all-reduce.10.cloned.1.call-start = ((), (), s32[]{:S(2)}) async-start(), calls=%async_computation.3 | async-start | bytes 3276800 | tf_op jit(solution)/shard_map/psum | solution.py:31
  202.6 92.8 %all-reduce.12.cloned.1.call-start = ((), (), s32[]{:S(2)}) async-start(), calls=%async_computation.4 | async-start | bytes 3276800 | tf_op jit(solution)/shard_map/psum | solution.py:31
  251.2 44.2 %copy-start.1 = (bf16[1,400,512]{2,1,0:T(8,128)(2,1)S(1)}, bf16[1,400,512]{2,1,0:T(8,128)(2,1)}, u32[]{:S(2)}) copy-start(bf16[1,400,512]{2,1,0:T(8,128)(2,1)} %param.6) | copy-start | bytes 1228804
Sparse Core Ops, SparseCore 0:
  9.5 22.7 all-gather.3
  109.4 39.9 all-reduce.5
  154.0 43.9 all-reduce.7
  202.7 43.9 all-reduce.9
  251.4 43.9 all-reduce.11
where the time goes:
time: 305 us; the launch traced here: 304 us
  waiting for transfers between devices  196 us (64%)
  blocking collectives  67.8 us (22%)
  matrix products  22 us (7%)
  between operations  13.8 us (5%)
    psum x4, waiting for transfers between devices, on_device(): term_whole = lax.psum(partial_value.astype(jnp.bfloat16), 'chol')  172 us
    unnamed x1, blocking collectives  35.5 us
    all_gather x1, blocking collectives, on_device(): all_weights = lax.all_gather(weights, 'walk', axis=0, tiled=True)  26.2 us
    all_gather x1, waiting for transfers between devices, on_device(): piece = lax.all_gather(orbitals, 'chol', axis=2, tiled=True)  23.1 us
    dot_general x4, matrix products, on_device(): jnp.einsum('wnp,mp->wnm', mixed, interp, preferred_element_type=jnp.float32)  18 us
    psum x1, blocking collectives, on_device(): force_bias = lax.psum(partial_bias, 'chol')  6.12 us
  transfers between devices with their start and end apart: 5, of which 5 were waited for; matrix products, arithmetic and copies ran while one was open for 0% of the time, Pallas kernels for 0%

commit v1 on v0

--- a/solution.py
+++ b/solution.py
@@ -28,7 +28,9 @@
     for order in range(1, TERMS + 1):
         mixed = (current * scales[:, None, :] / order).astype(jnp.bfloat16)
         partial_value = jnp.einsum("wnp,mp->wnm", mixed, interp, preferred_element_type=jnp.float32)
-        term_whole = lax.psum(partial_value.astype(jnp.bfloat16), "chol")
+        term_whole = jnp.sum(
+            lax.all_gather(partial_value.astype(jnp.bfloat16), axis_name="chol"), axis=0
+        )
         offset = lax.axis_index("chol") * basis_here
         term_local = lax.dynamic_slice_in_dim(term_whole, offset, basis_here, 2)
         total = total + term_local.astype(jnp.float32)

time: 305 us -> 344 us (1.13)
  other arithmetic: 2.4 us -> 25.8 us
  waiting for transfers between devices: 196 us -> 212 us
    all_gather x0 -> x4, waiting for transfers between devices: none -> 188 us  [on_device(): lax.all_gather(partial_value.astype(jnp.bfloat16), axis_name='chol')]
    psum x4 -> x0, waiting for transfers between devices: 172 us -> none  [on_device(): term_whole = lax.psum(partial_value.astype(jnp.bfloat16), 'chol')]
    reduce_sum x0 -> x4, other arithmetic: none -> 23.4 us  [on_device(): jnp.sum(lax.all_gather(partial_value.astype(jnp.bfloat16), axis_name='cho...]
where the time goes in v1:
time: 344 us; the launch traced here: 343 us
  waiting for transfers between devices  212 us (62%)
  blocking collectives  67.8 us (20%)
  other arithmetic  25.8 us (8%)
  matrix products  22.1 us (6%)
  between operations  13.8 us (4%)
    all_gather x4, waiting for transfers between devices, on_device(): lax.all_gather(partial_value.astype(jnp.bfloat16), axis_name='chol')  188 us
    unnamed x1, blocking collectives  35.5 us
    all_gather x1, blocking collectives, on_device(): all_weights = lax.all_gather(weights, 'walk', axis=0, tiled=True)  26.2 us
    reduce_sum x4, other arithmetic, on_device(): jnp.sum(lax.all_gather(partial_value.astype(jnp.bfloat16), axis_name='cho...  23.4 us
    all_gather x1, waiting for transfers between devices, on_device(): piece = lax.all_gather(orbitals, 'chol', axis=2, tiled=True)  23.1 us
    dot_general x4, matrix products, on_device(): jnp.einsum('wnp,mp->wnm', mixed, interp, preferred_element_type=jnp.float32)  18.1 us
  transfers between devices with their start and end apart: 5, of which 5 were waited for; matrix products, arithmetic and copies ran while one was open for 0% of the time, Pallas kernels for 0%

profile of v1, /device:TPU:0, one launch (start us, length us, event | category | flops | bytes accessed | tf_op | source)
XLA Modules:
  0.0 343.4 jit_solution(14299514259871961916)
XLA Ops:
  7.2 0.0 copy-start
  7.2 0.0 all-gather.12.cloned.1.call-start
  7.2 0.7 all-gather.12.cloned.1.call-update
  7.9 0.0 all-gather.14.cloned.1.call-start
  8.0 1.2 dynamic-slice.16
  9.2 0.0 copy-start.2
  9.2 0.0 copy-start.4
  9.2 23.1 %all-gather.12.cloned.1.call-done = bf16[1,400,2048]{2,1,0:T(8,128)(2,1)} async-done(((bf16[1,400,512]{2,1,0:T(8,128)(2,1)}), bf16[1,400,2048]{2,1,0:T(8,128)(2,1)}) %all-gather.12.cloned.1.call-update) | async-done | bytes 1638416 | tf_op jit(solution)/shard_map/all_gather | solution.py:12
  32.3 0.0 copy-done
  32.3 3.5 %fusion.15 = f32[512]{0:T(512)S(1)} fusion(bf16[2048,512]{1,0:T(8,128)(2,1)S(1)} %copy-done, bf16[1,400,2048]{2,1,0:T(8,128)(2,1)} %all-gather.12.cloned.1.call-done, bf16[400,512]{1,0:T(8,128)(2,1)} %param.9, bf16[1,400,400]{2,1,0:T(8,128)(2,1)} %param.7), kind=kOutput, calls=%fused_computation.20 | convolution fusion | flops 1495653888 | bytes 4467200 | tf_op jit(solution)/shard_map/wim,mp->wip/dot_general | solution.py:16
  35.8 26.2 %all-gather.5 = f32[8,1,512]{2,1,0:T(1,128)S(1)} all-gather(f32[1,1,512]{2,1,0:T(1,128)S(1)} %bitcast.57), channel_id=2, replica_groups=mesh['walk'=8,'chol'=4] {'walk'}, dimensions={0}, use_global_device_ids=true | all-gather | bytes 18432 | tf_op jit(solution)/shard_map/all_gather | solution.py:21
  62.0 0.0 copy-done.2
  62.0 0.2 fusion.30
  62.2 6.1 %psum.7 = f32[8,256]{1,0:T(8,128)S(1)} all-reduce(f32[8,256]{1,0:T(8,128)S(1)} %fusion.30), channel_id=1, replica_groups=mesh['walk'=8,'chol'=4] {'chol'}, use_global_device_ids=true, to_apply=%region_1.0 | all-reduce | flops 2048 | bytes 16384 | tf_op jit(solution)/shard_map/psum | solution.py:23
  68.3 0.0 copy-done.4
  68.3 0.0 copy-start.3
  68.3 0.3 fusion.33
  68.6 35.5 %all-reduce = f32[8,512]{1,0:T(8,128)S(1)} all-reduce(f32[8,512]{1,0:T(8,128)S(1)} %fusion.33), channel_id=7, replica_groups=mesh['walk'=8,'chol'=4] {'walk'}, use_global_device_ids=true, to_apply=%region_2.0.clone | all-reduce | flops 4096 | bytes 32768
  104.1 0.6 constant_dynamic-slice_fusion
  104.8 4.5 %convolution_convert_fusion.3 = bf16[400,2048]{1,0:T(8,128)(2,1)} fusion(bf16[2048,512]{1,0:T(8,128)(2,1)S(1)} %copy-done, bf16[1,400,2048]{2,1,0:T(8,128)(2,1)} %all-gather.12.cloned.1.call-done, f32[512]{0:T(512)S(1)} %bitcast.58), kind=kOutput, calls=%fused_computation.3 | convolution fusion | flops 1678950400 | bytes 5376000 | tf_op jit(solution)/shard_map/wnp,mp->wnm/dot_general | solution.py:30
  109.3 0.0 copy-done.3
  109.3 0.0 all-gather.14.cloned.1.call-update
  109.3 0.0 all-gather.16.cloned.1.call-start
  109.4 44.0 %all-gather.14.cloned.1.call-done = bf16[1600,2048]{1,0:T(8,128)(2,1)} async-done(((bf16[400,2048]{1,0:T(8,128)(2,1)}), bf16[1600,2048]{1,0:T(8,128)(2,1)}) %all-gather.14.cloned.1.call-update) | async-done | bytes 6553616 | tf_op jit(solution)/shard_map/all_gather | solution.py:32
  153.3 5.8 %reduce.10 = bf16[400,2048]{1,0:T(8,128)(2,1)} reduce(bf16[4,400,2048]{2,1,0:T(8,128)(2,1)} %bitcast.54, bf16[]{:T(256)} %constant.9.clone.1), dimensions={0}, to_apply=%region_3.0 | reduce | flops 2457600 | bytes 8192002 | tf_op jit(solution)/shard_map/reduce_sum | solution.py:31
  159.1 4.6 %convolution_convert_fusion.2 = bf16[400,2048]{1,0:T(8,128)(2,1)} fusion(bf16[2048,512]{1,0:T(8,128)(2,1)S(1)} %copy-done, bf16[400,2048]{1,0:T(8,128)(2,1)} %reduce.10, f32[512]{0:T(512)S(1)} %bitcast.59), kind=kOutput, calls=%fused_computation.2 | convolution fusion | flops 1679155200 | bytes 5376000 | tf_op jit(solution)/shard_map/wnp,mp->wnm/dot_general | solution.py:30
  163.7 0.0 all-gather.16.cloned.1.call-update
  163.8 0.0 all-gather.18.cloned.1.call-start
  163.8 48.0 %all-gather.16.cloned.1.call-done = bf16[1600,2048]{1,0:T(8,128)(2,1)} async-done(((bf16[400,2048]{1,0:T(8,128)(2,1)}), bf16[1600,2048]{1,0:T(8,128)(2,1)}) %all-gather.16.cloned.1.call-update) | async-done | bytes 6553616 | tf_op jit(solution)/shard_map/all_gather | solution.py:32
  211.8 5.9 %reduce.11 = bf16[400,2048]{1,0:T(8,128)(2,1)} reduce(bf16[4,400,2048]{2,1,0:T(8,128)(2,1)} %bitcast.55, bf16[]{:T(256)} %constant.9.clone.1), dimensions={0}, to_apply=%region_4.0 | reduce | flops 2457600 | bytes 8192002 | tf_op jit(solution)/shard_map/reduce_sum | solution.py:31
  217.7 4.5 %convolution_convert_fusion.1 = bf16[400,2048]{1,0:T(8,128)(2,1)} fusion(bf16[2048,512]{1,0:T(8,128)(2,1)S(1)} %copy-done, bf16[400,2048]{1,0:T(8,128)(2,1)} %reduce.11, f32[512]{0:T(512)S(1)} %bitcast.60), kind=kOutput, calls=%fused_computation.1 | convolution fusion | flops 1679155200 | bytes 5376000 | tf_op jit(solution)/shard_map/wnp,mp->wnm/dot_general | solution.py:30
  222.2 0.0 all-gather.18.cloned.1.call-update
  222.2 0.2 all-gather.20.cloned.1.call-start
  222.4 47.8 %all-gather.18.cloned.1.call-done = bf16[1600,2048]{1,0:T(8,128)(2,1)} async-done(((bf16[400,2048]{1,0:T(8,128)(2,1)}), bf16[1600,2048]{1,0:T(8,128)(2,1)}) %all-gather.18.cloned.1.call-update) | async-done | bytes 6553616 | tf_op jit(solution)/shard_map/all_gather | solution.py:32
  270.2 5.8 %reduce.12 = bf16[400,2048]{1,0:T(8,128)(2,1)} reduce(bf16[4,400,2048]{2,1,0:T(8,128)(2,1)} %bitcast.56, bf16[]{:T(256)} %constant.9.clone.1), dimensions={0}, to_apply=%region_5.0 | reduce | flops 2457600 | bytes 8192002 | tf_op jit(solution)/shard_map/reduce_sum | solution.py:31
  276.0 4.5 %convolution_convert_fusion = bf16[400,2048]{1,0:T(8,128)(2,1)} fusion(bf16[2048,512]{1,0:T(8,128)(2,1)S(1)} %copy-done, bf16[400,2048]{1,0:T(8,128)(2,1)} %reduce.12, f32[512]{0:T(512)S(1)} %bitcast.61), kind=kOutput, calls=%fused_computation | convolution fusion | flops 1679155200 | bytes 5376000 | tf_op jit(solution)/shard_map/wnp,mp->wnm/dot_general | solution.py:30
  280.6 0.0 all-gather.20.cloned.1.call-update
  280.6 48.0 %all-gather.20.cloned.1.call-done = bf16[1600,2048]{1,0:T(8,128)(2,1)} async-done(((bf16[400,2048]{1,0:T(8,128)(2,1)}), bf16[1600,2048]{1,0:T(8,128)(2,1)}) %all-gather.20.cloned.1.call-update) | async-done | bytes 6553616 | tf_op jit(solution)/shard_map/all_gather | solution.py:32
  328.6 0.0 copy-start.1
  328.6 5.9 %reduce.13 = bf16[400,2048]{1,0:T(8,128)(2,1)} reduce(bf16[4,400,2048]{2,1,0:T(8,128)(2,1)} %bitcast.53, bf16[]{:T(256)} %constant.9.clone.1), dimensions={0}, to_apply=%region_6.0 | reduce | flops 2457600 | bytes 8192002 | tf_op jit(solution)/shard_map/reduce_sum | solution.py:31
  334.4 0.0 copy-done.1
  334.4 2.4 fusion.18
Async XLA Ops:
  7.2 25.1 %copy-start = (bf16[2048,512]{1,0:T(8,128)(2,1)S(1)}, bf16[2048,512]{1,0:T(8,128)(2,1)}, u32[]{:S(2)}) copy-start(bf16[2048,512]{1,0:T(8,128)(2,1)} %param.8) | copy-start | bytes 6291460
  7.2 25.1 %all-gather.12.cloned.1.call-start = ((), (), s32[]{:S(2)}) async-start(), calls=%async_computation | async-start | bytes 2048000 | tf_op jit(solution)/shard_map/all_gather | solution.py:12
  7.9 145.4 %all-gather.14.cloned.1.call-start = ((), (), s32[]{:S(2)}) async-start(), calls=%async_computation.1 | async-start | bytes 8192000 | tf_op jit(solution)/shard_map/all_gather | solution.py:32
  9.2 52.8 %copy-start.2 = (bf16[512,256]{1,0:T(8,128)(2,1)S(1)}, bf16[512,256]{1,0:T(8,128)(2,1)}, u32[]{:S(2)}) copy-start(bf16[512,256]{1,0:T(8,128)(2,1)} %param.10) | copy-start | bytes 786436
  9.2 59.1 %copy-start.4 = (f32[8,256]{1,0:T(8,128)S(1)}, f32[8,256]{1,0:T(8,128)}, u32[]{:S(2)}) copy-start(f32[8,256]{1,0:T(8,128)} %param.11) | copy-start | bytes 24580
  68.3 41.0 %copy-start.3 = (f32[8,256]{1,0:T(8,128)}, f32[8,256]{1,0:T(8,128)S(1)}, u32[]{:S(2)}) copy-start(f32[8,256]{1,0:T(8,128)S(1)} %psum.7) | copy-start | bytes 24580
  109.3 102.4 %all-gather.16.cloned.1.call-start = ((), (), s32[]{:S(2)}) async-start(), calls=%async_computation.2 | async-start | bytes 8192000 | tf_op jit(solution)/shard_map/all_gather | solution.py:32
  163.8 106.4 %all-gather.18.cloned.1.call-start = ((), (), s32[]{:S(2)}) async-start(), calls=%async_computation.3 | async-start | bytes 8192000 | tf_op jit(solution)/shard_map/all_gather | solution.py:32
  222.2 106.4 %all-gather.20.cloned.1.call-start = ((), (), s32[]{:S(2)}) async-start(), calls=%async_computation.4 | async-start | bytes 8192000 | tf_op jit(solution)/shard_map/all_gather | solution.py:32
  328.6 5.9 %copy-start.1 = (bf16[1,400,512]{2,1,0:T(8,128)(2,1)S(1)}, bf16[1,400,512]{2,1,0:T(8,128)(2,1)}, u32[]{:S(2)}) copy-start(bf16[1,400,512]{2,1,0:T(8,128)(2,1)} %param.6) | copy-start | bytes 1228804
Sparse Core Ops, SparseCore 0:
  9.5 22.7 all-gather.11
  109.4 43.8 all-gather.13
  163.9 47.8 all-gather.15
  222.3 47.8 all-gather.17
  280.7 47.8 all-gather.19
